TPU v7x, 256 devices: a whole 4x4x8 slice. The times are simulated.
256 devices in a mesh: clip: 32 (over z_lo, x, core), tm: 8 (over y, z_hi).
Axes of the slice: x: 4, y: 4, z: 8 (z_hi: 2, z_lo: 4; z = z_hi * 4 + z_lo), core: 2. Of those that a mesh axis runs over, the one named last changes fastest.
Arguments:
- block_input: bfloat16 [32, 16, 32, 4096], P('clip', 'tm'), may hold values from -6 to 6
- input_cache: bfloat16 [32, 2, 32, 4096], P('clip'), may hold values from -6 to 6
- middle_cache: bfloat16 [32, 2, 32, 4096], P('clip'), may hold values from -6 to 6
- first_weight: bfloat16 [3, 3, 3, 64, 64], replicated, may hold values from -0.15625 to 0.15625
- first_bias: float32 [64], replicated, may hold values from -3 to 3
- second_weight: bfloat16 [3, 3, 3, 64, 64], replicated, may hold values from -0.15625 to 0.15625
- cotangent: bfloat16 [32, 16, 32, 4096], P('clip', 'tm'), may hold values from -6 to 6
Outputs:
- input_grad: bfloat16 [32, 16, 32, 4096], P('clip', 'tm')
- input_cache_grad: bfloat16 [32, 2, 32, 4096], P('clip', None, 'tm')
- middle_cache_grad: bfloat16 [32, 2, 32, 4096], P('clip', None, 'tm')
- first_weight_grad: float32 [3, 3, 3, 64, 64], replicated
- second_weight_grad: float32 [3, 3, 3, 64, 64], replicated
All inputs are finite; a program needn't handle non-finite values.
Results may differ from a plain program's by a relative error of at most 0.009.
Values may be sent and summed in bfloat16 or wider, within the bound.
A program may use at most 128 MiB of HBM per device.

v0:
```python
import math

import jax
import jax.numpy as jnp
from jax import lax
from jax.sharding import PartitionSpec as P


def from_behind(block, axis, distance):
    devices = range(lax.axis_size(axis))
    route = [(i - distance, i) for i in devices if i - distance in devices]
    return lax.ppermute(block, axis, route)


def rows_for(lines, devices):
    spare = -lines.shape[0] % devices
    if not spare:
        return lines
    return jnp.concatenate([lines, jnp.zeros((spare, *lines.shape[1:]), lines.dtype)])


def spread(array, axis, root):
    lines = jnp.where(lax.axis_index(axis) == root, array, jnp.zeros_like(array)).reshape(
        -1, *array.shape[1:][-1:]
    )
    padded = rows_for(lines, lax.axis_size(axis))
    own = lax.psum_scatter(padded, axis, scatter_dimension=0, tiled=True)
    return lax.all_gather(own, axis, axis=0, tiled=True)[: len(lines)].reshape(array.shape)


def to_cells(array, chans):
    return array.reshape(
        array.shape[0], array.shape[1], array.shape[2], array.shape[3] // chans, chans
    )


def to_rows(array):
    return array.reshape(
        array.shape[0], array.shape[1], array.shape[2], array.shape[3] * array.shape[4]
    )


def conv_forward(source, weight, row_pad):
    chans = weight.shape[3]
    result = lax.conv_general_dilated(
        to_cells(source, chans),
        weight,
        (1, 1, 1),
        ((0, 0), (row_pad, row_pad), (1, 1)),
        dimension_numbers=("NDHWC", "DHWIO", "NDHWC"),
        preferred_element_type=jnp.float32,
    )
    return to_rows(result)


def conv_input_grad(upstream, weight, row_pad):
    chans = weight.shape[3]
    flipped = jnp.transpose(jnp.flip(weight, (0, 1, 2)), (0, 1, 2, 4, 3))
    result = lax.conv_general_dilated(
        to_cells(upstream, chans),
        flipped,
        (1, 1, 1),
        ((2, 2), (row_pad, row_pad), (1, 1)),
        dimension_numbers=("NDHWC", "DHWIO", "NDHWC"),
        preferred_element_type=jnp.float32,
    )
    return to_rows(result)


def conv_weight_grad(source, upstream, chans, row_pad):
    return lax.conv_general_dilated(
        to_cells(source, chans),
        to_cells(upstream, chans),
        (1, 1, 1),
        ((0, 0), (row_pad, row_pad), (1, 1)),
        dimension_numbers=("CDHWN", "IDHWO", "DHWNC"),
        preferred_element_type=jnp.float32,
    )


def silu_slope(value):
    logistic = jax.nn.sigmoid(value)
    return logistic * (1.0 + value * (1.0 - logistic))


def first_layer(extended, weight, bias_row):
    activated = jax.nn.silu(extended.astype(jnp.float32)).astype(jnp.bfloat16)
    pre = conv_forward(activated, weight, 1) + bias_row
    return (activated, pre, jax.nn.silu(pre).astype(jnp.bfloat16))


def body(
    block_input, input_cache, middle_cache, first_weight, first_bias, second_weight, cotangent
):
    chans = first_weight.shape[3]
    width = block_input.shape[3] // chans
    bias_row = jnp.tile(first_bias, width)
    position = lax.axis_index("tm")
    count = (
        block_input.shape[0]
        * lax.axis_size("clip")
        * block_input.shape[1]
        * lax.axis_size("tm")
        * block_input.shape[2]
        * width
    )
    factor = 1.0 / math.sqrt(count)
    band = block_input.shape[2] // lax.axis_size("tm")
    offset = position * band
    second_total = None
    at_start = position == 0
    prev_input = from_behind(block_input, "tm", 1)
    left_input = jnp.where(at_start, input_cache, prev_input)
    extended = jnp.concatenate([left_input, block_input], axis=1)
    activated, pre, middle = first_layer(extended, first_weight, bias_row)
    far_input = from_behind(block_input, "tm", 2)
    far_input = jnp.where(position == 1, input_cache, far_input)
    unused_act, unused_pre, prev_middle = first_layer(
        jnp.concatenate([far_input, prev_input], axis=1), first_weight, bias_row
    )
    left_middle = jnp.where(at_start, middle_cache, prev_middle)
    middle_ext = jnp.concatenate([left_middle, middle], axis=1)
    middle_ext_grad = conv_input_grad(cotangent, second_weight, 1)
    second_sum = conv_weight_grad(middle_ext, cotangent, chans, 1) * factor
    from_next = from_behind(middle_ext_grad[:, :2].astype(jnp.bfloat16), "tm", -1).astype(
        jnp.float32
    )
    own_middle = middle_ext_grad[:, 2:]
    middle_grad = jnp.concatenate([own_middle[:, :-2], own_middle[:, -2:] + from_next], axis=1)
    pre_grad = (middle_grad * silu_slope(pre)).astype(jnp.bfloat16)
    activated_grad = conv_input_grad(pre_grad, first_weight, 1)
    first_sum = conv_weight_grad(activated, pre_grad, chans, 1) * factor
    extended_grad = activated_grad * silu_slope(extended.astype(jnp.float32))
    from_after = from_behind(extended_grad[:, :2].astype(jnp.bfloat16), "tm", -1).astype(
        jnp.float32
    )
    own_input = cotangent.astype(jnp.float32) + extended_grad[:, 2:]
    input_grad = jnp.concatenate(
        [own_input[:, :-2], own_input[:, -2:] + from_after], axis=1
    ).astype(jnp.bfloat16)
    whole_input_cache, whole_middle_cache = (
        spread(extended_grad[:, :2].astype(jnp.bfloat16), "tm", 0),
        spread(middle_ext_grad[:, :2].astype(jnp.bfloat16), "tm", 0),
    )
    input_cache_grad = lax.dynamic_slice_in_dim(whole_input_cache, offset, band, 2)
    middle_cache_grad = lax.dynamic_slice_in_dim(whole_middle_cache, offset, band, 2)
    first_total, second_total = lax.psum((first_sum, second_sum), ("clip", "tm"))
    return (input_grad, input_cache_grad, middle_cache_grad, first_total, second_total)


def solution(mesh):
    return jax.shard_map(
        body,
        mesh=mesh,
        in_specs=(
            P("clip", "tm", None, None),
            P("clip", None, None, None),
            P("clip", None, None, None),
            P(),
            P(),
            P(),
            P("clip", "tm", None, None),
        ),
        out_specs=(
            P("clip", "tm", None, None),
            P("clip", None, "tm", None),
            P("clip", None, "tm", None),
            P(),
            P(),
        ),
        check_vma=False,
    )
```

profile of v0, /device:TPU:2, one launch (start us, length us, event | category | flops | bytes accessed | tf_op | source)
XLA Modules:
  0.0 503.7 jit_solution(7840904377907799492)
XLA Ops:
  8.1 10.0 %collective-permute-start.1 = (bf16[1,2,32,4096]{3,2,1,0:T(8,128)(2,1)}, bf16[1,2,32,4096]{3,2,1,0:T(8,128)(2,1)}, u32[]{:S(2)}, u32[]{:S(2)}) collective-permute-start(bf16[1,2,32,4096]{3,2,1,0:T(8,128)(2,1)} %param.7), channel_id=1, source_target_pairs={{0,1},{1,2},{2,3},{3,4},{4,5},{5,6},{6,7},{8,9},{9,10},{10,11},{11... | collective-permute-start | bytes 1572872 | tf_op jit(solution)/shard_map/ppermute | solution.py:12
  18.1 3.5 collective-permute-start.3
  21.6 2.1 reshape.366
  25.4 17.9 %broadcast_select_fusion.1 = f32[4,32,8,9,64]{4,2,3,1,0:T(8,128)S(1)} fusion(pred[8,9]{0,1:T(8,128)(4,1)S(1)} %copy-done.18, bf16[3,3,3,64,64]{4,3,2,1,0:T(8,128)(2,1)S(1)} %copy-done.17, bf16[2,32,1,7,2,64]{5,3,4,1,0,2:T(8,128)(2,1)S(1)} %slice.29, bf16[2,32,1,8,9,64]{5,3,4,1,0,2:T(8,128)(2,1)S(1)} %copy.41), kind=kOutput, calls=%fused_computation.38 | convolution fusion | flops 1000734720 | bytes 3285064 | tf_op jit(solution)/shard_map/conv_general_dilated | solution.py:59
  44.6 4.4 copy.43
  49.0 3.5 reshape.327
  55.5 2.1 concatenate.48
  57.6 3.9 reshape.395
  61.7 1.9 broadcast_select_fusion.2
  68.8 5.8 %multiply_convert_fusion = (bf16[2,32,8,9,64]{4,2,3,1,0:T(8,128)(2,1)}, f32[2,32,8,9,64]{4,2,3,1,0:T(8,128)S(1)}) fusion(f32[64]{0:T(128)S(1)} %copy-done.16, bf16[3,3,3,64,64]{4,3,2,1,0:T(8,128)(2,1)S(1)} %copy-done, bf16[4,32,1,7,2,64]{5,3,4,1,0,2:T(8,128)(2,1)S(1)} %slice.33, bf16[4,32,1,8,9,64]{5,3,4,1,0,2:T(8,128)(2,1)S(1)} %copy.46, ...), kind=kOutput, calls=%fused_computation.36 | convolution fusion | flops 1004371968 | bytes 3400008 | tf_op jit(solution)/shard_map/conv_general_dilated | solution.py:45
  75.3 2.5 copy.48
  77.8 3.4 reshape.328
  81.2 2.5 fusion.5
  85.2 2.1 reshape.378
  87.3 3.7 reshape.394
  92.2 2.1 concatenate.52
  98.2 4.8 fusion.36
  106.6 2.1 copy.70
  109.4 17.8 %broadcast_select_fusion = f32[4,32,8,9,64]{4,2,3,1,0:T(8,128)S(1)} fusion(pred[8,9]{0,1:T(8,128)(4,1)S(1)} %copy-done.18, bf16[3,3,3,64,64]{4,3,2,1,0:T(8,128)(2,1)S(1)} %copy-done, bf16[2,32,1,7,2,64]{5,3,4,1,0,2:T(8,128)(2,1)S(1)} %slice.35, bf16[2,32,1,8,9,64]{5,3,4,1,0,2:T(8,128)(2,1)S(1)} %copy.51), kind=kOutput, calls=%fused_computation.37 | convolution fusion | flops 1000734720 | bytes 3285064 | tf_op jit(solution)/shard_map/conv_general_dilated | solution.py:59
  128.5 4.4 copy.53
  132.9 3.5 reshape.330
  136.4 1.8 fusion.34
  140.6 1.7 collective-permute-start.2
  142.4 28.5 %fusion.56 = f32[3,3,3,64,64]{4,3,2,1,0:T(8,128)} fusion(bf16[1,2,32,64,64]{4,0,3,2,1:T(2,128)(2,1)} %reshape.394, bf16[1,4,32,64,64]{4,3,2,1,0:T(8,128)(2,1)} %fusion.5), kind=kOutput, calls=%fused_computation.60 | convolution fusion | flops 877965312 | bytes 2015232 | tf_op jit(solution)/shard_map/conv_general_dilated | solution.py:71
  172.3 3.7 concatenate.60
  176.4 3.7 copy.64
  180.2 37.3 %fusion.59 = f32[3,3,3,64,64]{4,3,2,1,0:T(8,128)} fusion(bf16[1,2,32,64,64]{4,0,3,2,1:T(2,128)(2,1)S(1)} %copy-done.10, bf16[1,2,32,64,64]{4,0,3,2,1:T(2,128)(2,1)} %copy.64, bf16[1,2,32,64,64]{4,0,3,2,1:T(2,128)(2,1)} %concatenate.60), kind=kOutput, calls=%fused_computation.61 | convolution fusion | flops 880062464 | bytes 2015232 | tf_op jit(solution)/shard_map/conv_general_dilated | solution.py:71
  217.5 53.8 %all_gather.7 = bf16[64,4096]{1,0:T(8,128)(2,1)S(1)} all-gather(bf16[8,4096]{1,0:T(8,128)(2,1)} %reduce-scatter.5.cloned.1.call-done), channel_id=1, replica_groups=mesh['clip'=32,'tm'=8] {'tm'}, dimensions={0}, use_global_device_ids=true | all-gather | bytes 589824 | tf_op jit(solution)/shard_map/all_gather | solution.py:28
  272.0 2.2 fusion.61
  274.2 45.4 %all_gather.6 = bf16[64,4096]{1,0:T(8,128)(2,1)S(1)} all-gather(bf16[8,4096]{1,0:T(8,128)(2,1)} %reduce-scatter.3.cloned.1.call-done), channel_id=1, replica_groups=mesh['clip'=32,'tm'=8] {'tm'}, dimensions={0}, use_global_device_ids=true | all-gather | bytes 589824 | tf_op jit(solution)/shard_map/all_gather | solution.py:28
  320.3 172.4 %all-reduce.3.cloned.1.call-done = (f32[3,3,3,64,64]{4,3,2,1,0:T(8,128)}, f32[3,3,3,64,64]{4,3,2,1,0:T(8,128)}) async-done(((f32[3,3,3,64,64]{4,3,2,1,0:T(8,128)}, f32[3,3,3,64,64]{4,3,2,1,0:T(8,128)}), (f32[3,3,3,64,64]{4,3,2,1,0:T(8,128)}, f32[3,3,3,64,64]{4,3,2,1,0:T(8,128)})) %all-reduce.3.cloned.1.call-update) | async-done | bytes 884752 | tf_op jit(solution)/shard_map/psum | solution.py:147
  492.7 2.3 copy.78
  (91 shorter events, 30.3 us)
Async XLA Ops:
  8.0 60.8 %copy-start = (bf16[3,3,3,64,64]{4,3,2,1,0:T(8,128)(2,1)S(1)}, bf16[3,3,3,64,64]{4,3,2,1,0:T(8,128)(2,1)}, u32[]{:S(2)}) copy-start(bf16[3,3,3,64,64]{4,3,2,1,0:T(8,128)(2,1)} %param.10) | copy-start | bytes 663556
  8.0 209.5 %reduce-scatter.5.cloned.1.call-start = ((), (), s32[]{:S(2)}) async-start(), calls=%async_computation.3 | async-start | bytes 589824 | tf_op jit(solution)/shard_map/reduce_scatter | solution.py:27
  8.1 53.6 %collective-permute-start.1 = (bf16[1,2,32,4096]{3,2,1,0:T(8,128)(2,1)}, bf16[1,2,32,4096]{3,2,1,0:T(8,128)(2,1)}, u32[]{:S(2)}, u32[]{:S(2)}) collective-permute-start(bf16[1,2,32,4096]{3,2,1,0:T(8,128)(2,1)} %param.7), channel_id=1, source_target_pairs={{0,1},{1,2},{2,3},{3,4},{4,5},{5,6},{6,7},{8,9},{9,10},{10,11},{11... | collective-permute-start | bytes 1572872 | tf_op jit(solution)/shard_map/ppermute | solution.py:12
  18.1 43.6 %collective-permute-start.3 = (bf16[1,2,32,4096]{3,2,1,0:T(8,128)(2,1)}, bf16[1,2,32,4096]{3,2,1,0:T(8,128)(2,1)}, u32[]{:S(2)}, u32[]{:S(2)}) collective-permute-start(bf16[1,2,32,4096]{3,2,1,0:T(8,128)(2,1)} %param.7), channel_id=1, source_target_pairs={{0,2},{1,3},{2,4},{3,5},{4,6},{5,7},{8,10},{9,11},{10,12},{11,13},... | collective-permute-start | bytes 1572872 | tf_op jit(solution)/shard_map/ppermute | solution.py:12
  24.3 1.0 copy-start.17
  24.4 1.0 copy-start.18
  52.5 1.7 copy-start.2
  52.5 5.1 %copy-start.6 = (bf16[1,2,32,4096]{3,2,1,0:T(8,128)(2,1)S(1)}, bf16[1,2,32,4096]{3,2,1,0:T(8,128)(2,1)}, u32[]{:S(2)}) copy-start(bf16[1,2,32,4096]{3,2,1,0:T(8,128)(2,1)} %param.13) | copy-start | bytes 1572868
  53.6 7.9 %copy-start.16 = (f32[64]{0:T(128)S(1)}, f32[64]{0:T(128)}, u32[]{:S(2)}) copy-start(f32[64]{0:T(128)} %param.11) | copy-start | bytes 772
  53.6 220.6 %reduce-scatter.3.cloned.1.call-start = ((), (), s32[]{:S(2)}) async-start(), calls=%async_computation.2 | async-start | bytes 589824 | tf_op jit(solution)/shard_map/reduce_scatter | solution.py:27
  54.2 29.5 %collective-permute-start = (bf16[1,2,32,4096]{3,2,1,0:T(8,128)(2,1)}, bf16[1,2,32,4096]{3,2,1,0:T(8,128)(2,1)}, u32[]{:S(2)}, u32[]{:S(2)}) collective-permute-start(bf16[1,2,32,4096]{3,2,1,0:T(8,128)(2,1)} %get-tuple-element.8), channel_id=1, source_target_pairs={{1,0},{2,1},{3,2},{4,3},{5,4},{6,5},{7,6},{9,8},{10,9},{11,10},{12... | collective-permute-start | bytes 1572872 | tf_op jit(solution)/shard_map/ppermute | solution.py:12
  55.5 6.2 %copy-start.13 = (bf16[1,2,32,4096]{3,2,1,0:T(8,128)(2,1)S(1)}, bf16[1,2,32,4096]{3,2,1,0:T(8,128)(2,1)}, u32[]{:S(2)}) copy-start(bf16[1,2,32,4096]{3,2,1,0:T(8,128)(2,1)} %param.8) | copy-start | bytes 1572868
  61.6 22.0 %copy-start.14 = (f32[4096]{0:T(1024)}, f32[4096]{0:T(1024)S(1)}, u32[]{:S(2)}) copy-start(f32[4096]{0:T(1024)S(1)} %add.146) | copy-start | bytes 49156
  81.2 2.5 copy-start.3
  81.2 2.5 copy-start.7
  85.2 5.9 %copy-start.9 = (bf16[1,2,32,4096]{3,2,1,0:T(8,128)(2,1)S(1)}, bf16[1,2,32,4096]{3,2,1,0:T(8,128)(2,1)}, u32[]{:S(2)}) copy-start(bf16[1,2,32,4096]{3,2,1,0:T(8,128)(2,1)} %get-tuple-element.11) | copy-start | bytes 1572868
  138.2 1.3 copy-start.4
  140.6 131.4 %collective-permute-start.2 = (bf16[1,2,32,4096]{3,2,1,0:T(8,128)(2,1)}, bf16[1,2,32,4096]{3,2,1,0:T(8,128)(2,1)}, u32[]{:S(2)}, u32[]{:S(2)}) collective-permute-start(bf16[1,2,32,4096]{3,2,1,0:T(8,128)(2,1)} %get-tuple-element.10), channel_id=1, source_target_pairs={{1,0},{2,1},{3,2},{4,3},{5,4},{6,5},{7,6},{9,8},{10,9},{11,10},{12... | collective-permute-start | bytes 1572872 | tf_op jit(solution)/shard_map/ppermute | solution.py:12
  142.4 28.5 %copy-start.8 = (f32[1,2,32,4096]{3,2,1,0:T(8,128)S(1)}, f32[1,2,32,4096]{3,2,1,0:T(8,128)}, u32[]{:S(2)}) copy-start(f32[1,2,32,4096]{3,2,1,0:T(8,128)} %reshape.335) | copy-start | bytes 3145732
  142.4 28.5 %copy-start.15 = (f32[4096]{0:T(1024)S(1)}, f32[4096]{0:T(1024)}, u32[]{:S(2)}) copy-start(f32[4096]{0:T(1024)} %copy-done.14) | copy-start | bytes 49156
  170.9 5.2 %copy-start.11 = (bf16[2,32,8,9,64]{4,2,3,1,0:T(8,128)(2,1)S(1)}, bf16[2,32,8,9,64]{4,2,3,1,0:T(8,128)(2,1)}, u32[]{:S(2)}) copy-start(bf16[2,32,8,9,64]{4,2,3,1,0:T(8,128)(2,1)} %get-tuple-element.13) | copy-start | bytes 1769476
  176.3 3.8 copy-start.10
  180.1 312.6 %all-reduce.3.cloned.1.call-start = ((), (), s32[]{:S(2)}) async-start(), calls=%async_computation.4 | async-start | bytes 3538944 | tf_op jit(solution)/shard_map/psum | solution.py:147
  217.5 54.5 %copy-start.5 = (f32[1,4,32,4096]{3,2,1,0:T(8,128)S(1)}, f32[1,4,32,4096]{3,2,1,0:T(8,128)}, u32[]{:S(2)}) copy-start(f32[1,4,32,4096]{3,2,1,0:T(8,128)} %copy-done.4) | copy-start | bytes 6291460
  272.0 223.9 %copy-start.1 = (bf16[3,3,3,64,64]{4,3,2,1,0:T(8,128)(2,1)S(1)}, bf16[3,3,3,64,64]{4,3,2,1,0:T(8,128)(2,1)}, u32[]{:S(2)}) copy-start(bf16[3,3,3,64,64]{4,3,2,1,0:T(8,128)(2,1)} %param.10) | copy-start | bytes 663556
  492.7 2.3 copy-start.12
Sparse Core Ops, SparseCore 0:
  53.8 89.7 reduce-scatter.4
  180.2 89.8 reduce-scatter.2
Sparse Core Ops, SparseCore 1:
  217.6 275.1 all-reduce.2
where the time goes:
time: 514 us; the launch traced here: 504 us
  waiting for transfers between devices  172 us (33%)
  matrix products  112 us (22%)
  blocking collectives  99.2 us (19%)
  local copies, waits for them, and re-layouts  71.1 us (14%)
  starting transfers between devices  16.7 us (3%)
  between operations  16.4 us (3%)
  other arithmetic  15.7 us (3%)
    psum x1, waiting for transfers between devices, body(): lax.psum((first_sum, second_sum), ('clip', 'tm'))  172 us
    all_gather x2, blocking collectives, spread(): lax.all_gather(own, axis, axis=0, tiled=True)[:len(lines)]  99.2 us
    conv_general_dilated x2, matrix products, conv_weight_grad(): lax.conv_general_dilated(to_cells(source, chans), to_cells(upstream, chan...  65.8 us
    conv_general_dilated x2, matrix products, conv_input_grad(): lax.conv_general_dilated(to_cells(upstream, chans), flipped, (1, 1, 1), (...  35.8 us
    ppermute x4, starting transfers between devices, from_behind(): return lax.ppermute(block, axis, route)  16.6 us
    conv_general_dilated x10, local copies, waits for them, and re-layouts, conv_input_grad(): lax.conv_general_dilated(to_cells(upstream, chans), flipped, (1, 1, 1), (...  12.4 us
    reshape x6, local copies, waits for them, and re-layouts, to_cells(): array.reshape(array.shape[0], array.shape[1], array.shape[2], array.shape...  12.2 us
    reshape x4, local copies, waits for them, and re-layouts, to_rows(): array.reshape(array.shape[0], array.shape[1], array.shape[2], array.shape...  12.1 us
  transfers between devices with their start and end apart: 7, of which 1 were waited for; matrix products, arithmetic and copies ran while one was open for 38% of the time, Pallas kernels for 0%

commit v1 on v0

v1 whole, which is shorter than its diff:
```python
import functools
import math

import jax
import jax.numpy as jnp
from jax import lax
from jax.experimental import pallas as pl
from jax.experimental.pallas import tpu as pltpu
from jax.sharding import PartitionSpec as P

F32, BF16 = jnp.float32, jnp.bfloat16
MESH = pl.DeviceIdType.MESH
ROWS, PAIRS, OWN = 32, 17, 16
SPAN, HALF = PAIRS * 128, OWN * 128
FLAT = PAIRS * ROWS
KEEP = OWN * ROWS
TAPS = 27
ZLO, XS, CORES, YS = 4, 4, 2, 4
PLANE, LINE = XS * YS, ZLO * 2
SUMS = 28 * 64
PART = SUMS // CORES
PIECE = PART // PLANE


def widen(wide, weight):
    def step(k):
        kt, kr = k // 3, k % 3
        none = jnp.zeros((64, 64), BF16)
        taps = [none] + [weight[3 * k + kq] for kq in range(3)] + [none]
        columns = pl.ds(pl.multiple_of(128 * kr, 128), 128)
        for a in range(4):
            block = jnp.concatenate([taps[a + 1], taps[a]], axis=1)
            wide[pl.ds(pl.multiple_of(256 * kt + 64 * a, 64), 64), columns] = block

    loop(0, 9, step)


def widen_back(wide, weight):
    def step(k):
        kt, kr = k // 3, k % 3
        none = jnp.zeros((64, 64), BF16)
        taps = [none] + [weight[3 * (8 - k) + 2 - kq] for kq in range(3)] + [none]
        for b in range(2):
            rows = pl.ds(pl.multiple_of(128 * kr + 64 * b, 64), 64)
            for a in range(0, 4, 2):
                block = jnp.concatenate([taps[a + 1 - b], taps[a + 2 - b]], axis=1)
                wide[rows, pl.ds(pl.multiple_of(256 * kt + 64 * a, 128), 128)] = block

    loop(0, 9, step)


def silu_slope(value):
    logistic = jax.nn.sigmoid(value)
    return logistic * (1.0 + value * (1.0 - logistic))


def row_of(shape):
    return lax.broadcasted_iota(jnp.int32, shape, 0) % ROWS


def row_before(block):
    return jnp.where(row_of(block.shape) == 0, 0.0, pltpu.roll(block, 1, axis=0))


def row_after(block):
    return jnp.where(row_of(block.shape) == ROWS - 1, 0.0, pltpu.roll(block, block.shape[0] - 1, axis=0))


def half_shift(block):
    turn = pltpu.roll(block, 64, axis=1)
    none = jnp.zeros((ROWS, 128), F32)
    lane = lax.broadcasted_iota(jnp.int32, (FLAT + ROWS, 128), 1)
    return jnp.where(lane < 64, jnp.concatenate([none, turn], 0), jnp.concatenate([turn, none], 0)).astype(BF16)


def flat(ref, slot):
    return jnp.concatenate([ref[slot, :, 128 * l : 128 * l + 128] for l in range(PAIRS)], axis=0).astype(F32)


def conv(ref, slot, weight, back=True):
    parts = []
    for j in range(3):
        parts += [ref[slot + j, 0:FLAT, :], ref[slot + j, ROWS : FLAT + ROWS, :]]
    over = (((1,), (1 if back else 0,)), ((), ()))
    sums = lax.dot_general(jnp.concatenate(parts, axis=1), weight[...], over, preferred_element_type=F32)
    return sums[:, 128:256] + row_before(sums[:, 0:128]) + row_after(sums[:, 256:384])


def three_rows(ref, slot, block):
    ref[slot, 0] = row_after(block).astype(BF16)
    ref[slot, 1] = block.astype(BF16)
    ref[slot, 2] = row_before(block).astype(BF16)


def loop(low, high, step):
    def body(i, carry):
        step(i)
        return carry

    lax.fori_loop(low, high, body, 0)


def kernel(
    factor,
    x_hbm, icache_hbm, mcache_hbm, ct_hbm, weight1, weight2, bias,
    out, icg, mcg, grad1, grad2,
    x, ct, mc, acts, cts, mid3, slope, pg, pg3, pgs, eg, icp, mcp, raw1, raw2,
    w1, w2t, w1t, vsum, from_core, part, plane_out, plane_in, line, whole,
    core_sem, plane_send, plane_recv, line_send, line_recv, spread_send, spread_recv,
    local_sem, send_sem, recv_sem, piece_send, piece_recv, own_sem,
):
    tm = lax.axis_index("tm")
    four, side = tm // 2, tm % 2
    first, last = four == 0, four == 3
    other = tm + 1 - 2 * side
    clip = lax.axis_index("clip")
    zlo, across, core = clip // (XS * CORES), (clip // CORES) % XS, clip % CORES
    spot, depth = across * YS + four, zlo * 2 + side

    def in_plane(i):
        to = (spot + i) % PLANE
        return to, {"clip": (zlo * XS + to // YS) * CORES + core, "tm": to % YS * 2 + side}

    def in_line(i):
        to = (depth + i) % LINE
        return {"clip": (to // 2 * XS + across) * CORES + core, "tm": four * 2 + to % 2}

    def anyone(src, dst, send, recv, to):
        return pltpu.make_async_remote_copy(src, dst, send, recv, device_id=to, device_id_type=MESH)

    twin = {"clip": clip + 1 - 2 * core, "tm": tm}
    mine = pl.ds(pl.multiple_of(side * (15 * 128), 128), SPAN)
    theirs = pl.ds(pl.multiple_of((1 - side) * (15 * 128), 128), SPAN)
    keep = pl.ds(pl.multiple_of(side * 128, 128), HALF)
    home = pl.ds(pl.multiple_of(side * HALF, 128), HALF)

    def remote(src, dst, i, to):
        return pltpu.make_async_remote_copy(
            src, dst, send_sem.at[i], recv_sem.at[i], device_id={"tm": to}, device_id_type=MESH
        )

    here = []
    for f in range(2):
        here.append(pltpu.make_async_copy(x_hbm.at[f, :, mine], x.at[2 + 2 * side + f], local_sem.at[f]))
        here.append(pltpu.make_async_copy(ct_hbm.at[f, :, mine], ct.at[2 * side + f], local_sem.at[2 + f]))
    for copy in here:
        copy.start()
    cached = []
    for f in range(2):
        cached.append(pltpu.make_async_copy(icache_hbm.at[f, :, mine], x.at[f], local_sem.at[4 + f]))
        cached.append(pltpu.make_async_copy(mcache_hbm.at[f, :, mine], mc.at[f], local_sem.at[6 + f]))

    @pl.when(first)
    def _():
        for copy in cached:
            copy.start()

    barrier = pltpu.get_barrier_semaphore()
    for d in range(1, 8):
        pl.semaphore_signal(barrier, inc=1, device_id={"tm": (tm + d) % 8}, device_id_type=MESH)
    greeted = 8
    pl.semaphore_signal(barrier, inc=1, device_id=twin, device_id_type=MESH)
    for i in range(1, XS):
        for j in range(YS):
            to = {"clip": (zlo * XS + (across + i) % XS) * CORES + core, "tm": (four + j) % YS * 2 + side}
            pl.semaphore_signal(barrier, inc=1, device_id=to, device_id_type=MESH)
            greeted += 1
    for i in range(1, ZLO):
        for j in range(2):
            to = {"clip": ((zlo + i) % ZLO * XS + across) * CORES + core, "tm": four * 2 + (side + j) % 2}
            pl.semaphore_signal(barrier, inc=1, device_id=to, device_id_type=MESH)
            greeted += 1
    pl.semaphore_wait(barrier, greeted)

    x_swap = [remote(x_hbm.at[f, :, theirs], x.at[2 + 2 * side + f], f, other) for f in range(2)]
    ct_swap = [remote(ct_hbm.at[f, :, theirs], ct.at[2 * side + f], 2 + f, other) for f in range(2)]
    x_halo = [remote(x.at[4 + f], x.at[f], 4 + f, (tm + 2) % 8) for f in range(2)]
    ct_halo = [remote(ct.at[f], ct.at[4 + f], 6 + f, (tm + 6) % 8) for f in range(2)]
    pg_halo = [remote(pg.at[f], pg.at[4 + f], 8 + f, (tm + 6) % 8) for f in range(2)]
    for copy in x_swap + ct_swap:
        copy.start()
    for copy in here:
        copy.wait()

    @pl.when((side == 1) & jnp.logical_not(last))
    def _():
        for copy in x_halo:
            copy.start()

    @pl.when((side == 0) & jnp.logical_not(first))
    def _():
        for copy in ct_halo:
            copy.start()

    def activate(s):
        acts[s] = half_shift(jax.nn.silu(flat(x, s)))

    widen(w1, weight1)
    widen_back(w2t, weight2)
    widen_back(w1t, weight1)
    two_biases = jnp.concatenate([bias[...], bias[...]], axis=1)
    vsum[64 * TAPS :, :] = jnp.zeros((64, 128), F32)
    raw1[...] = jnp.zeros_like(raw1)
    raw2[...] = jnp.zeros_like(raw2)
    for s in range(2):
        cts[s] = jnp.zeros((FLAT + ROWS, 128), BF16)
        pgs[s] = jnp.zeros((FLAT + ROWS, 128), BF16)
    for f in range(2):
        x_swap[f].wait_recv()

        @pl.when((side == 0) & jnp.logical_not(last))
        def _():
            x_halo[f].start()

    loop(2, 6, activate)

    @pl.when(first)
    def _():
        for copy in cached:
            copy.wait()

    @pl.when(jnp.logical_not(first))
    def _():
        for copy in x_halo:
            copy.wait_recv()

    loop(0, 2, activate)

    def forward(t):
        pre = conv(acts, t, w1, False) + two_biases
        slope[t] = silu_slope(pre)
        three_rows(mid3, t + 2, jax.nn.silu(pre).astype(BF16).astype(F32))

    loop(0, 4, forward)

    @pl.when(first)
    def _():
        loop(0, 2, lambda s: three_rows(mid3, s, flat(mc, s)))

    for f in range(2):
        ct_swap[f].wait_recv()

        @pl.when((side == 1) & jnp.logical_not(first))
        def _():
            ct_halo[f].start()

    def shift_ct(s):
        cts[s + 2] = half_shift(flat(ct, s))

    def pre_gradient(n):
        grad = (conv(cts, n, w2t) * slope[n - 2]).astype(BF16)
        pg[n - 2] = grad
        grad = grad.astype(F32)
        three_rows(pg3, n - 2, grad)
        pgs[n] = half_shift(grad)

    loop(0, 4, shift_ct)
    loop(2, 4, pre_gradient)

    @pl.when(last)
    def _():
        for s in range(6, 8):
            cts[s] = jnp.zeros((FLAT + ROWS, 128), BF16)

    @pl.when(jnp.logical_not(last))
    def _():
        for copy in ct_halo:
            copy.wait_recv()
        loop(4, 6, shift_ct)

    @pl.when(jnp.logical_not(first))
    def _():
        for copy in pg_halo:
            copy.start()

    loop(4, 6, pre_gradient)

    def pieces(ref, f, block):
        wide = jnp.concatenate([block[ROWS * l : ROWS * l + ROWS, :] for l in range(PAIRS)], axis=1)
        for p in range(8):
            ref[p, f] = wide[4 * p : 4 * p + 4, :].astype(BF16)

    def deal(ref, result, k, start):
        for p in range(8):
            far = pltpu.make_async_remote_copy(
                ref.at[p, :, :, keep], result.at[:, :, home], piece_send.at[k, p], piece_recv.at[k, side],
                device_id={"tm": p}, device_id_type=MESH,
            )
            near = pltpu.make_async_copy(ref.at[p, :, :, keep], result.at[:, :, home], own_sem.at[k])

            @pl.when(first & (tm != p))
            def _():
                far.start() if start else far.wait_send()

            @pl.when(first & (tm == p))
            def _():
                near.start() if start else near.wait()

    def dealt(ref, result, k):
        for s in range(2):
            columns = pl.ds(s * HALF, HALF)

            @pl.when(tm != s)
            def _():
                pltpu.make_async_remote_copy(
                    ref.at[0, :, :, pl.ds(0, HALF)], result.at[:, :, columns], piece_send.at[k, 0], piece_recv.at[k, s],
                    device_id={"tm": tm}, device_id_type=MESH,
                ).wait_recv()

    @pl.when(first)
    def _():
        loop(0, 2, lambda n: pieces(mcp, n, conv(cts, n, w2t)))

    deal(mcp, mcg, 0, True)

    own = pl.ds(pl.multiple_of(side * ROWS, ROWS), KEEP)
    next_own = pl.ds(pl.multiple_of(side * ROWS + ROWS, ROWS), KEEP)

    def operands(still, still_slot, moved, moved_slot):
        one = jnp.concatenate([still[still_slot, v, own, :] for v in range(3)], axis=1)
        parts = []
        for j in range(3):
            parts += [moved[moved_slot + j, own, :], moved[moved_slot + j, next_own, :]]
        return one, jnp.concatenate(parts, axis=1)

    over_rows = (((0,), (0,)), ((), ()))

    def second_sum(n):
        one, four_px = operands(mid3, n, cts, n)
        raw2[...] += lax.dot_general(one, four_px, over_rows, preferred_element_type=F32)

    def first_sum(t):
        one, four_px = operands(pg3, t, acts, t)
        raw1[...] += lax.dot_general(four_px, one, over_rows, preferred_element_type=F32)

    loop(jnp.where(first, 0, 2), 6, second_sum)
    loop(0, 4, first_sum)
    lane = lax.broadcasted_iota(jnp.int32, (64, 128), 1)
    for kt in range(3):
        for kr in range(3):
            one = 128 * kr
            two = 128 * (2 - kr)
            low = raw2[two : two + 64, 256 * (2 - kt) : 256 * (3 - kt)]
            high = raw2[two + 64 : two + 128, 256 * (2 - kt) : 256 * (3 - kt)]
            second = low + pltpu.roll(high, 192, axis=1)
            for kq in range(3):
                at = 256 * kt + 64 * kq
                tap = (kt * 3 + kr) * 3 + kq
                left = raw1[at : at + 64, one : one + 128]
                left += pltpu.roll(raw1[at + 64 : at + 128, one : one + 128], 64, axis=1)
                right = second[:, 128 * ((2 - kq) // 2) : 128 * ((2 - kq) // 2) + 128]
                if kq != 1:
                    right = pltpu.roll(right, 64, axis=1)
                vsum[64 * tap : 64 * tap + 64, :] = jnp.where(lane < 64, left, right)

    half_of = lambda c: pl.ds(pl.multiple_of(c * PART, 8), PART)
    cores = anyone(vsum.at[half_of(1 - core)], from_core, core_sem.at[0], core_sem.at[1], twin)
    cores.start()

    @pl.when(last)
    def _():
        for s in range(6, 8):
            pgs[s] = jnp.zeros((FLAT + ROWS, 128), BF16)

    def shift_pg(s):
        pgs[s + 2] = half_shift(pg[s].astype(F32))

    @pl.when(jnp.logical_not(last))
    def _():
        for copy in pg_halo:
            copy.wait_recv()
        loop(4, 6, shift_pg)

    def extended_gradient(n):
        return conv(pgs, n, w1t) * silu_slope(flat(x, n))

    def input_gradient(i):
        t = (2 * (1 - side) + i) % 4
        block = extended_gradient(t + 2) + flat(ct, t)
        for l in range(PAIRS):
            eg[i, :, 128 * l : 128 * l + 128] = block[ROWS * l : ROWS * l + ROWS, :].astype(BF16)

    back = [remote(eg.at[f, :, keep], out.at[f, :, home], 10 + f, other) for f in range(2)]
    stay = [pltpu.make_async_copy(eg.at[2 + f, :, keep], out.at[f, :, home], local_sem.at[f]) for f in range(2)]
    loop(0, 1, input_gradient)
    cores.wait_recv()
    part[...] = vsum[half_of(core), :] + from_core[...]
    plane_out[...] = part[...].reshape(PLANE, PIECE, 128).astype(BF16)
    loop(1, 2, input_gradient)
    gathers = []
    for i in range(1, PLANE):
        to, device = in_plane(i)
        gathers.append(anyone(plane_out.at[to], plane_in.at[i], plane_send.at[i], plane_recv.at[i], device))
    for copy in gathers + back:
        copy.start()
    loop(2, 4, input_gradient)

    @pl.when(first)
    def _():
        loop(0, 2, lambda n: pieces(icp, n, extended_gradient(n)))

    for copy in stay:
        copy.start()
    total = part[pl.ds(pl.multiple_of(spot * PIECE, 8), PIECE), :]
    for i, copy in enumerate(gathers):
        copy.wait_recv()
        total += plane_in[i + 1].astype(F32)
    line[depth] = total.astype(BF16)
    deal(icp, icg, 1, True)
    lines = [anyone(line.at[depth], line.at[depth], line_send.at[i], line_recv.at[i], in_line(i)) for i in range(1, LINE)]
    for copy in lines:
        copy.start()
    for copy in lines:
        copy.wait_recv()
    total = line[0].astype(F32)
    for i in range(1, LINE):
        total += line[i].astype(F32)
    whole[core, spot] = (total * factor).astype(BF16)
    spreads = []
    for i in range(1, PLANE):
        to, device = in_plane(i)
        spreads.append(anyone(whole.at[core, spot], whole.at[core, spot], spread_send.at[i], spread_recv.at[i], device))
    for copy in spreads:
        copy.start()
    for copy in spreads:
        copy.wait_recv()
    twins = anyone(whole.at[core], whole.at[core], core_sem.at[2], core_sem.at[3], twin)
    twins.start()
    twins.wait_recv()
    sums = whole[...].astype(F32).reshape(SUMS, 128)
    for tap in range(TAPS):
        block = sums[64 * tap : 64 * tap + 64, :]
        grad1[tap] = block[:, 0:64]
        grad2[tap] = pltpu.roll(block, 64, axis=1)[:, 0:64]

    for copy in stay:
        copy.wait()
    for copy in x_swap + ct_swap + [cores, twins] + gathers + lines + spreads:
        copy.wait_send()

    @pl.when(jnp.logical_not(last))
    def _():
        for copy in x_halo:
            copy.wait_send()

    @pl.when(jnp.logical_not(first))
    def _():
        for copy in ct_halo + pg_halo:
            copy.wait_send()

    for copy in back:
        copy.wait()
    deal(mcp, mcg, 0, False)
    deal(icp, icg, 1, False)
    dealt(mcp, mcg, 0)
    dealt(icp, icg, 1)


def body(block_input, input_cache, middle_cache, first_weight, first_bias, second_weight, cotangent):
    count = 1024 * lax.axis_size("clip") * lax.axis_size("tm") * 4
    anywhere = pl.BlockSpec(memory_space=pl.ANY)
    inside = pl.BlockSpec(memory_space=pltpu.VMEM)
    out, icg, mcg, grad1, grad2 = pl.pallas_call(
        functools.partial(kernel, 1.0 / math.sqrt(count)),
        out_shape=(
            jax.ShapeDtypeStruct((2, ROWS, 4096), BF16),
            jax.ShapeDtypeStruct((2, 4, 4096), BF16),
            jax.ShapeDtypeStruct((2, 4, 4096), BF16),
            jax.ShapeDtypeStruct((TAPS, 64, 64), F32),
            jax.ShapeDtypeStruct((TAPS, 64, 64), F32),
        ),
        in_specs=[anywhere] * 4 + [inside] * 3,
        out_specs=(anywhere, anywhere, anywhere, inside, inside),
        scratch_shapes=[
            pltpu.VMEM((6, ROWS, SPAN), BF16),
            pltpu.VMEM((6, ROWS, SPAN), BF16),
            pltpu.VMEM((2, ROWS, SPAN), BF16),
            pltpu.VMEM((6, FLAT + ROWS, 128), BF16),
            pltpu.VMEM((8, FLAT + ROWS, 128), BF16),
            pltpu.VMEM((6, 3, FLAT, 128), BF16),
            pltpu.VMEM((4, FLAT, 128), F32),
            pltpu.VMEM((6, FLAT, 128), BF16),
            pltpu.VMEM((4, 3, FLAT, 128), BF16),
            pltpu.VMEM((8, FLAT + ROWS, 128), BF16),
            pltpu.VMEM((4, ROWS, SPAN), BF16),
            pltpu.VMEM((8, 2, 4, SPAN), BF16),
            pltpu.VMEM((8, 2, 4, SPAN), BF16),
            pltpu.VMEM((768, 384), F32),
            pltpu.VMEM((384, 768), F32),
            pltpu.VMEM((768, 384), BF16),
            pltpu.VMEM((384, 768), BF16),
            pltpu.VMEM((384, 768), BF16),
            pltpu.VMEM((SUMS, 128), F32),
            pltpu.VMEM((PART, 128), F32),
            pltpu.VMEM((PART, 128), F32),
            pltpu.VMEM((PLANE, PIECE, 128), BF16),
            pltpu.VMEM((PLANE, PIECE, 128), BF16),
            pltpu.VMEM((LINE, PIECE, 128), BF16),
            pltpu.VMEM((CORES, PLANE, PIECE, 128), BF16),
            pltpu.SemaphoreType.DMA((4,)),
            pltpu.SemaphoreType.DMA((PLANE,)),
            pltpu.SemaphoreType.DMA((PLANE,)),
            pltpu.SemaphoreType.DMA((LINE,)),
            pltpu.SemaphoreType.DMA((LINE,)),
            pltpu.SemaphoreType.DMA((PLANE,)),
            pltpu.SemaphoreType.DMA((PLANE,)),
            pltpu.SemaphoreType.DMA((8,)),
            pltpu.SemaphoreType.DMA((12,)),
            pltpu.SemaphoreType.DMA((12,)),
            pltpu.SemaphoreType.DMA((2, 8)),
            pltpu.SemaphoreType.DMA((2, 2)),
            pltpu.SemaphoreType.DMA((2,)),
        ],
        compiler_params=pltpu.CompilerParams(
            collective_id=0, has_side_effects=True, vmem_limit_bytes=56 << 20
        ),
    )(
        block_input[0], input_cache[0], middle_cache[0], cotangent[0],
        first_weight.reshape(TAPS, 64, 64), second_weight.reshape(TAPS, 64, 64), first_bias.reshape(1, 64),
    )
    shape = (3, 3, 3, 64, 64)
    return (out[None], icg[None], mcg[None], grad1.reshape(shape), grad2.reshape(shape))


def solution(mesh):
    return jax.shard_map(
        body,
        mesh=mesh,
        in_specs=(
            P("clip", "tm", None, None),
            P("clip", None, None, None),
            P("clip", None, None, None),
            P(),
            P(),
            P(),
            P("clip", "tm", None, None),
        ),
        out_specs=(
            P("clip", "tm", None, None),
            P("clip", None, "tm", None),
            P("clip", None, "tm", None),
            P(),
            P(),
        ),
        check_vma=False,
    )
```

time: 514 us -> 91.4 us (0.18)
  the two profiles are of different devices: /device:TPU:2 before, /device:TPU:1 now
where the time goes in v1:
time: 91.4 us; the launch traced here: 91.1 us
  Pallas kernels  84.6 us (93%)
  local copies, waits for them, and re-layouts  5.86 us (6%)
    pallas_call x1, Pallas kernels, body(): pl.pallas_call(functools.partial(kernel, 1.0 / math.sqrt(count)), out_sha...  84.6 us
    unnamed x13, local copies, waits for them, and re-layouts  5.86 us

profile of v1, /device:TPU:1, one launch (start us, length us, event | category | flops | bytes accessed | tf_op | source)
XLA Modules:
  0.0 91.1 jit_solution(17737353677897137453)
XLA Ops:
  0.6 84.6 %shard_map.110 = (bf16[2,32,4096]{2,1,0:T(8,128)(2,1)}, bf16[2,4,4096]{2,1,0:T(4,128)(2,1)}, bf16[2,4,4096]{2,1,0:T(4,128)(2,1)}, f32[27,64,64]{2,1,0:T(8,128)}, f32[27,64,64]{2,1,0:T(8,128)}) custom-call(bf16[2,32,4096]{2,1,0:T(8,128)(2,1)} %bitcast.14, bf16[2,32,4096]{2,1,0:T(8,128)(2,1)} %bitcast.15, bf16[2,32,4096]{2,1,0:T(8,128)(2,1)} %bitcast.16, ...), custom_call_target="tpu_custom_call" | custom-call | tf_op jit(solution)/shard_map/pallas_call | solution.py:463
  85.2 0.0 copy-start.1
  85.2 0.0 copy-start.3
  85.2 2.0 %copy.17 = bf16[1,2,32,4096]{3,2,1,0:T(8,128)(2,1)} copy(bf16[1,2,32,4096]{3,2,1,0:T(8,128)(2,1)} %bitcast.18) | data formatting | bytes 1048576
  87.2 0.0 copy-done.3
  87.2 0.0 copy-start.2
  87.2 0.6 copy.18
  87.8 0.2 copy-done.2
  88.1 0.6 copy.19
  88.7 0.0 copy-done.1
  88.7 0.0 copy-start
  88.7 0.9 %copy.20 = f32[3,3,3,64,64]{4,3,2,1,0:T(8,128)} copy(f32[3,3,3,64,64]{4,3,2,1,0:T(8,128)S(1)} %bitcast.13) | data formatting | bytes 884736
  89.6 0.6 copy-done
  90.2 0.9 copy.21
Async XLA Ops:
  85.2 3.5 %copy-start.1 = (f32[27,64,64]{2,1,0:T(8,128)S(1)}, f32[27,64,64]{2,1,0:T(8,128)}, u32[]{:S(2)}) copy-start(f32[27,64,64]{2,1,0:T(8,128)} %get-tuple-element.13) | copy-start | bytes 1327108
  85.2 2.0 %copy-start.3 = (bf16[2,4,4096]{2,1,0:T(4,128)(2,1)S(1)}, bf16[2,4,4096]{2,1,0:T(4,128)(2,1)}, u32[]{:S(2)}) copy-start(bf16[2,4,4096]{2,1,0:T(4,128)(2,1)} %get-tuple-element.11) | copy-start | bytes 196612
  87.2 0.9 copy-start.2
  88.7 1.5 %copy-start = (f32[27,64,64]{2,1,0:T(8,128)S(1)}, f32[27,64,64]{2,1,0:T(8,128)}, u32[]{:S(2)}) copy-start(f32[27,64,64]{2,1,0:T(8,128)} %get-tuple-element.14) | copy-start | bytes 1327108

commit v2 on v1

v2 whole, which is shorter than its diff:
```python
import functools
import math

import jax
import jax.numpy as jnp
from jax import lax
from jax.experimental import pallas as pl
from jax.experimental.pallas import tpu as pltpu
from jax.sharding import PartitionSpec as P

F32, BF16 = jnp.float32, jnp.bfloat16
MESH = pl.DeviceIdType.MESH
ROWS, PAIRS, OWN = 32, 17, 16
SPAN, HALF = PAIRS * 128, OWN * 128
FLAT = PAIRS * ROWS
KEEP = OWN * ROWS
TAPS = 27
ARRIVE = ((0, 5), (5, 9), (9, 13), (13, 17))
FOLLOW = ((0, 4), (4, 8), (8, 12), (12, 17))
SETTLE = ((0, 3), (3, 7), (7, 11), (11, 16))
ZLO, XS, CORES, YS = 4, 4, 2, 4
PLANE, LINE = XS * YS, ZLO * 2
SUMS = 28 * 64
PART = SUMS // CORES
PIECE = PART // PLANE


def widen(wide, weight):
    def step(k):
        kt, kr = k // 3, k % 3
        none = jnp.zeros((64, 64), BF16)
        taps = [none] + [weight[3 * k + kq] for kq in range(3)] + [none]
        columns = pl.ds(pl.multiple_of(128 * kr, 128), 128)
        for a in range(4):
            block = jnp.concatenate([taps[a + 1], taps[a]], axis=1)
            wide[pl.ds(pl.multiple_of(256 * kt + 64 * a, 64), 64), columns] = block

    loop(0, 9, step)


def widen_back(wide, weight):
    def step(k):
        kt, kr = k // 3, k % 3
        none = jnp.zeros((64, 64), BF16)
        taps = [none] + [weight[3 * (8 - k) + 2 - kq] for kq in range(3)] + [none]
        for b in range(2):
            rows = pl.ds(pl.multiple_of(128 * kr + 64 * b, 64), 64)
            for a in range(0, 4, 2):
                block = jnp.concatenate([taps[a + 1 - b], taps[a + 2 - b]], axis=1)
                wide[rows, pl.ds(pl.multiple_of(256 * kt + 64 * a, 128), 128)] = block

    loop(0, 9, step)


def silu_slope(value):
    logistic = jax.nn.sigmoid(value)
    return logistic * (1.0 + value * (1.0 - logistic))


def row_of(shape):
    return lax.broadcasted_iota(jnp.int32, shape, 0) % ROWS


def row_before(block):
    return jnp.where(row_of(block.shape) == 0, 0.0, pltpu.roll(block, 1, axis=0))


def row_after(block):
    return jnp.where(row_of(block.shape) == ROWS - 1, 0.0, pltpu.roll(block, block.shape[0] - 1, axis=0))


def half_shift(block, ends=True):
    none = jnp.zeros((ROWS, 128), F32)
    turn = pltpu.roll(block, 64, axis=1)
    left, right = (jnp.concatenate([none, turn], 0), jnp.concatenate([turn, none], 0)) if ends else (turn[:-ROWS], turn[ROWS:])
    lane = lax.broadcasted_iota(jnp.int32, left.shape, 1)
    return jnp.where(lane < 64, left, right).astype(BF16)


def piece_shift(load, low, high):
    none = jnp.zeros((ROWS, 128), F32)
    blocks = [load(l).astype(F32) if 0 <= l < PAIRS else none for l in range(low - 1, high + (high == PAIRS))]
    return half_shift(jnp.concatenate(blocks, 0), False)


def flat(ref, slot):
    return jnp.concatenate([ref[slot, :, 128 * l : 128 * l + 128] for l in range(PAIRS)], axis=0).astype(F32)


def conv(ref, slots, weight, back=True, low=0, high=PAIRS):
    frames = []
    for slot in slots:
        parts = []
        for j in range(3):
            parts += [ref[slot + j, ROWS * low : ROWS * high, :], ref[slot + j, ROWS * low + ROWS : ROWS * high + ROWS, :]]
        frames.append(jnp.concatenate(parts, axis=1))
    over = (((1,), (1 if back else 0,)), ((), ()))
    sums = lax.dot_general(jnp.concatenate(frames, axis=0), weight[...], over, preferred_element_type=F32)
    return sums[:, 128:256] + row_before(sums[:, 0:128]) + row_after(sums[:, 256:384])


def three_rows(ref, slot, block):
    ref[slot, 0] = row_after(block).astype(BF16)
    ref[slot, 1] = block.astype(BF16)
    ref[slot, 2] = row_before(block).astype(BF16)


def loop(low, high, step):
    def body(i, carry):
        step(i)
        return carry

    lax.fori_loop(low, high, body, 0)


def kernel(
    factor,
    x_hbm, icache_hbm, mcache_hbm, ct_hbm, weight1, weight2, bias,
    out, icg, mcg, sums,
    x, ct, mc, acts, cts, mid3, slope, mid_grad, pg, pg3, pgs, eg, dealt, passed, raw1, raw2,
    w1, w2t, w1t, vsum, from_core, plane_out, plane_in, line, whole,
    core_sem, plane_send, plane_recv, line_send, line_recv, spread_send, spread_recv, leave_sem,
    local_sem, send_sem, recv_sem, deal_sem, pass_send, pass_recv, own_sem,
):
    tm = lax.axis_index("tm")
    four, side = tm // 2, tm % 2
    first, last = four == 0, four == 3
    other = tm + 1 - 2 * side
    clip = lax.axis_index("clip")
    zlo, across, core = clip // (XS * CORES), (clip // CORES) % XS, clip % CORES
    spot, depth = across * YS + four, zlo * 2 + side

    def in_plane(i):
        to = (spot + i) % PLANE
        return to, {"clip": (zlo * XS + to // YS) * CORES + core, "tm": to % YS * 2 + side}

    def in_line(i):
        to = (depth + i) % LINE
        return {"clip": (to // 2 * XS + across) * CORES + core, "tm": four * 2 + to % 2}

    def anyone(src, dst, send, recv, to):
        return pltpu.make_async_remote_copy(src, dst, send, recv, device_id=to, device_id_type=MESH)

    twin = {"clip": clip + 1 - 2 * core, "tm": tm}
    mine = pl.ds(pl.multiple_of(side * (15 * 128), 128), SPAN)
    theirs = pl.ds(pl.multiple_of((1 - side) * (15 * 128), 128), SPAN)
    keep = pl.ds(pl.multiple_of(side * 128, 128), HALF)
    home = pl.ds(pl.multiple_of(side * HALF, 128), HALF)

    def remote(src, dst, i, to):
        return pltpu.make_async_remote_copy(
            src, dst, send_sem.at[i], recv_sem.at[i], device_id={"tm": to}, device_id_type=MESH
        )

    here = []
    for f in range(2):
        here.append(pltpu.make_async_copy(x_hbm.at[f, :, mine], x.at[2 + 2 * side + f], local_sem.at[f]))
        here.append(pltpu.make_async_copy(ct_hbm.at[f, :, mine], ct.at[2 * side + f], local_sem.at[2 + f]))
    for copy in here:
        copy.start()
    cached = []
    for f in range(2):
        cached.append(pltpu.make_async_copy(icache_hbm.at[f, :, mine], x.at[f], local_sem.at[4 + f]))
        cached.append(pltpu.make_async_copy(mcache_hbm.at[f, :, mine], mc.at[f], local_sem.at[6 + f]))

    @pl.when(first)
    def _():
        for copy in cached:
            copy.start()

    barrier = pltpu.get_barrier_semaphore()
    for d in range(1, 8):
        pl.semaphore_signal(barrier, inc=1, device_id={"tm": (tm + d) % 8}, device_id_type=MESH)
    greeted = 8
    pl.semaphore_signal(barrier, inc=1, device_id=twin, device_id_type=MESH)
    for i in range(1, XS):
        for j in range(YS):
            to = {"clip": (zlo * XS + (across + i) % XS) * CORES + core, "tm": (four + j) % YS * 2 + side}
            pl.semaphore_signal(barrier, inc=1, device_id=to, device_id_type=MESH)
            greeted += 1
    for i in range(1, ZLO):
        for j in range(2):
            to = {"clip": ((zlo + i) % ZLO * XS + across) * CORES + core, "tm": four * 2 + (side + j) % 2}
            pl.semaphore_signal(barrier, inc=1, device_id=to, device_id_type=MESH)
            greeted += 1
    pl.semaphore_wait(barrier, greeted)

    x_swap, ct_swap, x_halo, ct_halo, pg_halo = [], [], [], [], []
    for c, ((low, high), (a, b)) in enumerate(zip(ARRIVE, FOLLOW)):
        cut = pl.ds(pl.multiple_of((1 - side) * (15 * 128) + 128 * low, 128), 128 * (high - low))
        cols = pl.ds(128 * low, 128 * (high - low))
        rows = pl.ds(ROWS * a, ROWS * (b - a))
        ours, two, four_on = pl.ds(2 * side, 2), pl.ds(0, 2), pl.ds(4, 2)
        x_swap.append(remote(x_hbm.at[:, :, cut], x.at[pl.ds(2 + 2 * side, 2), :, cols], c, other))
        ct_swap.append(remote(ct_hbm.at[:, :, cut], ct.at[ours, :, cols], 4 + c, other))
        x_halo.append(remote(x.at[four_on, :, cols], x.at[two, :, cols], 8 + c, (tm + 2) % 8))
        ct_halo.append(remote(ct.at[two, :, cols], ct.at[four_on, :, cols], 12 + c, (tm + 6) % 8))
        pg_halo.append(remote(pg.at[two, rows, :], pg.at[four_on, rows, :], 16 + c, (tm + 6) % 8))

    @pl.when(side == 0)
    def _():
        for copy in ct_swap + x_swap:
            copy.start()

    @pl.when(side == 1)
    def _():
        for copy in x_swap + ct_swap:
            copy.start()

    for copy in here:
        copy.wait()

    @pl.when((side == 1) & jnp.logical_not(last))
    def _():
        for copy in x_halo:
            copy.start()

    @pl.when((side == 0) & jnp.logical_not(first))
    def _():
        for copy in ct_halo:
            copy.start()

    widen(w1, weight1)
    widen_back(w2t, weight2)
    widen_back(w1t, weight1)
    two_biases = jnp.concatenate([bias[...], bias[...]], axis=1)
    vsum[64 * TAPS :, :] = jnp.zeros((64, 128), F32)

    @pl.when(last)
    def _():
        for s in range(4, 6):
            ct[s] = jnp.zeros((ROWS, SPAN), BF16)
            pg[s] = jnp.zeros((FLAT, 128), BF16)

    for s in range(2):
        cts[s] = jnp.zeros((FLAT + ROWS, 128), BF16)
        pgs[s] = jnp.zeros((FLAT + ROWS, 128), BF16)
    raw2[...] = jnp.zeros_like(raw2)

    def forward(c):
        @pl.when(jnp.logical_not(first))
        def _():
            x_halo[c].wait_recv()

        (low, high), (a, b) = ARRIVE[c], FOLLOW[c]
        for s in range(6):
            acts[s, ROWS * low : ROWS * (high + (high == PAIRS)), :] = piece_shift(
                lambda l, s=s: jax.nn.silu(x[s, :, 128 * l : 128 * l + 128].astype(F32)), low, high
            )
        pre = conv(acts, range(4), w1, False, a, b) + two_biases
        slopes = silu_slope(pre)
        middle = jax.nn.silu(pre).astype(BF16)
        wide = middle.astype(F32)
        before, after = row_before(wide).astype(BF16), row_after(wide).astype(BF16)
        size = ROWS * (b - a)
        for t in range(4):
            here, there = slice(size * t, size * t + size), slice(ROWS * a, ROWS * b)
            slope[t, there, :] = slopes[here]
            mid3[t + 2, 0, there, :] = after[here]
            mid3[t + 2, 1, there, :] = middle[here]
            mid3[t + 2, 2, there, :] = before[here]

    over_rows = (((0,), (0,)), ((), ()))

    def operands(still, moved, frames, ahead, rows):
        one, four_px = [], []
        for n in frames:
            one.append(jnp.concatenate([still[n, v, rows[0], :] for v in range(3)], axis=1))
            four_px.append(jnp.concatenate([moved[n + ahead + j, r, :] for j in range(3) for r in rows], axis=1))
        return jnp.concatenate(one, axis=0), jnp.concatenate(four_px, axis=0)

    def own_rows(c):
        i, k = SETTLE[c]
        return [pl.ds(pl.multiple_of((side + e + i) * ROWS, ROWS), ROWS * (k - i)) for e in range(2)]

    def backward(c):
        @pl.when(jnp.logical_not(last))
        def _():
            ct_halo[c].wait_recv()

        (low, high), (a, b) = ARRIVE[c], FOLLOW[c]
        for s in range(6):
            cts[s + 2, ROWS * low : ROWS * (high + (high == PAIRS)), :] = piece_shift(
                lambda l, s=s: ct[s, :, 128 * l : 128 * l + 128], low, high
            )
        grad = conv(cts, range(2, 6), w2t, low=a, high=b)
        size = ROWS * (b - a)
        for t in range(4):
            mid_grad[t, ROWS * a : ROWS * b, :] = grad[size * t : size * t + size]

        @pl.when(first)
        def _():
            one, four_px = operands(mid3, cts, range(2), 0, own_rows(c))
            raw2[...] += lax.dot_general(one, four_px, over_rows, preferred_element_type=F32)

    def settle(c):
        a, b = FOLLOW[c]
        size = ROWS * (b - a)
        grad = jnp.concatenate([mid_grad[t, ROWS * a : ROWS * b, :] for t in range(4)], axis=0)
        grad = (grad * jnp.concatenate([slope[t, ROWS * a : ROWS * b, :] for t in range(4)], axis=0)).astype(BF16)
        wide = grad.astype(F32)
        before, after = row_before(wide).astype(BF16), row_after(wide).astype(BF16)
        for t in range(4):
            here, there = slice(size * t, size * t + size), slice(ROWS * a, ROWS * b)
            pg[t, there, :] = grad[here]
            pg3[t, 0, there, :] = after[here]
            pg3[t, 1, there, :] = grad[here]
            pg3[t, 2, there, :] = before[here]
            pgs[t + 2, ROWS * a : ROWS * (b + (b == PAIRS)), :] = piece_shift(
                lambda l, t=t: pg[t, ROWS * l : ROWS * l + ROWS, :], a, b
            )
        rows = own_rows(c)
        raw2[...] += lax.dot_general(*operands(mid3, cts, range(2, 6), 0, rows), over_rows, preferred_element_type=F32)
        one, four_px = operands(pg3, acts, range(4), 0, rows)
        sums = lax.dot_general(four_px, one, over_rows, preferred_element_type=F32)
        raw1[...] = sums if c == 0 else raw1[...] + sums

        @pl.when(jnp.logical_not(first))
        def _():
            pg_halo[c].start()

    @pl.when(first)
    def _():
        for copy in cached:
            copy.wait()
        loop(0, 2, lambda s: three_rows(mid3, s, flat(mc, s)))

    @pl.when(side == 0)
    def _():
        for c in range(5):
            if c < 4:
                x_swap[c].wait_recv()

                @pl.when(jnp.logical_not(last))
                def _():
                    x_halo[c].start()

            if c > 0:
                forward(c - 1)

    @pl.when(side == 1)
    def _():
        for c in range(5):
            if c < 4:
                ct_swap[c].wait_recv()

                @pl.when(jnp.logical_not(first))
                def _():
                    ct_halo[c].start()

            if c > 0:
                backward(c - 1)

    for c in range(4):
        @pl.when(side == 0)
        def _():
            ct_swap[c].wait_recv()
            backward(c)

        @pl.when(side == 1)
        def _():
            x_swap[c].wait_recv()
            forward(c)

        settle(c)

    def pieces(k, f, block):
        wide = jnp.concatenate([block[ROWS * l : ROWS * l + ROWS, :] for l in range(PAIRS)], axis=1)
        for p in range(8):
            dealt[p, k, f] = wide[4 * p : 4 * p + 4, :].astype(BF16)

    deals = []
    for v in range(1, YS):
        pair = dealt.at[pl.ds(2 * v, 2), :, :, :, keep]
        deals.append(anyone(pair, passed, deal_sem.at[v], deal_sem.at[0], {"tm": 2 * v + side}))

    def pass_on(held, act):
        for k, result in enumerate((mcg, icg)):
            to = result.at[:, :, home]
            near = pltpu.make_async_copy(held(side, k), to, own_sem.at[k])
            act(near, anyone(held(1 - side, k), to, pass_send.at[k], pass_recv.at[k], {"tm": other}))

    def pass_all(act):
        @pl.when(first)
        def _():
            pass_on(lambda q, k: dealt.at[q, k, :, :, keep], act)

        @pl.when(jnp.logical_not(first))
        def _():
            pass_on(lambda q, k: passed.at[q, k], act)

    def extended_gradient(n):
        return conv(pgs, [n], w1t) * silu_slope(flat(x, n))

    def input_gradient(t):
        block = extended_gradient(t + 2) + flat(ct, t)
        for l in range(PAIRS):
            eg[t, :, 128 * l : 128 * l + 128] = block[ROWS * l : ROWS * l + ROWS, :].astype(BF16)

    far = 2 - 2 * side
    back = [remote(eg.at[far + f, :, keep], out.at[f, :, home], 20 + f, other) for f in range(2)]
    stay = [pltpu.make_async_copy(eg.at[2 - far + f, :, keep], out.at[f, :, home], local_sem.at[f]) for f in range(2)]
    lane = lax.broadcasted_iota(jnp.int32, (64, 128), 1)

    def fold(taps):
        for tap in taps:
            kt, kr, kq = tap // 9, tap // 3 % 3, tap % 3
            at, one, two = 256 * kt + 64 * kq, 128 * kr, 128 * (2 - kr)
            left = raw1[at : at + 64, one : one + 128]
            left += pltpu.roll(raw1[at + 64 : at + 128, one : one + 128], 64, axis=1)
            at = 256 * (2 - kt)
            low, high = raw2[two : two + 64, at : at + 256], raw2[two + 64 : two + 128, at : at + 256]
            if kq == 1:
                right = low[:, 0:128] + pltpu.roll(high[:, 128:256], 64, axis=1)
            else:
                tile = 1 - kq // 2
                right = pltpu.roll(low[:, 128 * tile : 128 * tile + 128], 64, axis=1) + high[:, 128 * tile : 128 * tile + 128]
            vsum[64 * tap : 64 * tap + 64, :] = jnp.where(lane < 64, left, right)

    half_of = lambda c: pl.ds(pl.multiple_of(c * PART, 8), PART)
    cores = anyone(vsum.at[half_of(1 - core)], from_core, core_sem.at[0], core_sem.at[1], twin)
    for k in range(2):

        @pl.when(core == k)
        def _():
            fold(range(14 * (1 - k), min(TAPS, 28 - 14 * k)))
            cores.start()
            fold(range(14 * k, min(TAPS, 14 + 14 * k)))


    loop(0, 2, input_gradient)

    @pl.when(side == 1)
    def _():
        for copy in back:
            copy.start()

    cores.wait_recv()

    def part(to):
        own = pl.ds(pl.multiple_of(core * PART + to * PIECE, 8), PIECE)
        return vsum[own, :] + from_core[pl.ds(pl.multiple_of(to * PIECE, 8), PIECE), :]

    gathers = []
    for i in range(1, PLANE):
        to, device = in_plane(i)
        plane_out[i] = part(to).astype(BF16)
        gathers.append(anyone(plane_out.at[i], plane_in.at[i], plane_send.at[i], plane_recv.at[i], device))
        gathers[-1].start()
    @pl.when(jnp.logical_not(last))
    def _():
        for copy in pg_halo:
            copy.wait_recv()

    def shift_pg(s):
        pgs[s + 2] = half_shift(pg[s].astype(F32))

    loop(4, 6, shift_pg)
    loop(2, 3, input_gradient)

    @pl.when(side == 0)
    def _():
        back[0].start()

    loop(3, 4, input_gradient)

    @pl.when(side == 0)
    def _():
        back[1].start()

    for copy in stay:
        copy.start()
    @pl.when(first)
    def _():
        loop(0, 2, lambda n: pieces(0, n, conv(cts, [n], w2t)))
        loop(0, 2, lambda n: pieces(1, n, extended_gradient(n)))
        for copy in deals:
            copy.start()

    total = part(spot)
    for i, copy in enumerate(gathers):
        copy.wait_recv()
        total += plane_in[i + 1].astype(F32)
    line[depth] = total.astype(BF16)
    lines = [anyone(line.at[depth], line.at[depth], line_send.at[i], line_recv.at[i], in_line(i)) for i in range(1, LINE)]
    for copy in lines:
        copy.start()
    for copy in lines:
        copy.wait_recv()
    total = line[0].astype(F32)
    for i in range(1, LINE):
        total += line[i].astype(F32)
    whole[core, spot] = (total * factor).astype(BF16)
    spreads = []
    for i in range(1, PLANE):
        to, device = in_plane(i)
        spreads.append(anyone(whole.at[core, spot], whole.at[core, spot], spread_send.at[i], spread_recv.at[i], device))
    for copy in spreads:
        copy.start()

    @pl.when(jnp.logical_not(first))
    def _():
        deals[0].wait_recv()

    pass_all(lambda near, far: (near.start(), far.start()))
    for copy in spreads:
        copy.wait_recv()
    twins = anyone(whole.at[core], whole.at[core], core_sem.at[2], core_sem.at[3], twin)
    twins.start()
    leave = [pltpu.make_async_copy(whole.at[h], sums.at[h], leave_sem.at[e]) for e, h in enumerate((core, 1 - core))]
    leave[0].start()
    twins.wait_recv()
    leave[1].start()
    for copy in stay:
        copy.wait()
    for copy in x_swap + ct_swap + [cores, twins] + gathers + lines + spreads:
        copy.wait_send()

    @pl.when(jnp.logical_not(last))
    def _():
        for copy in x_halo:
            copy.wait_send()

    @pl.when(jnp.logical_not(first))
    def _():
        for copy in ct_halo + pg_halo:
            copy.wait_send()

    back[0].wait_recv()
    back[1].wait_recv()
    for copy in back:
        copy.wait_send()
    @pl.when(first)
    def _():
        for copy in deals:
            copy.wait_send()

    for copy in leave:
        copy.wait()
    pass_all(lambda near, far: (near.wait(), far.wait()))


def deliver(
    out_in, icg_in, mcg_in, sums_in, out, icg, mcg, grad1, grad2, out_at, icg_at, mcg_at, sums_at, one, two, in_sem, out_sem
):
    loads = [
        pltpu.make_async_copy(src, dst, in_sem.at[i])
        for i, (src, dst) in enumerate(((sums_in, sums_at), (out_in, out_at), (icg_in, icg_at), (mcg_in, mcg_at)))
    ]
    stores = [
        pltpu.make_async_copy(src, dst, out_sem.at[i])
        for i, (src, dst) in enumerate(((out_at, out), (icg_at, icg), (mcg_at, mcg)))
    ]
    for copy in loads:
        copy.start()
    loads[0].wait()
    for k in range(3):
        part = pl.ds(9 * k, 9)
        block = sums_at[...].astype(F32).reshape(SUMS, 128)[576 * k : 576 * k + 576]
        turned_block = pltpu.roll(block, 64, axis=1)
        for tap in range(9):
            one[9 * k + tap] = block[64 * tap : 64 * tap + 64, 0:64]
            two[9 * k + tap] = turned_block[64 * tap : 64 * tap + 64, 0:64]
        stores.append(pltpu.make_async_copy(one.at[part], grad1.at[part], out_sem.at[3 + 2 * k]))
        stores.append(pltpu.make_async_copy(two.at[part], grad2.at[part], out_sem.at[4 + 2 * k]))
        for copy in stores[-2:]:
            copy.start()
    for load, store in zip(loads[1:], stores[:3]):
        load.wait()
        store.start()
    for copy in stores:
        copy.wait()


def body(block_input, input_cache, middle_cache, first_weight, first_bias, second_weight, cotangent):
    count = 1024 * lax.axis_size("clip") * lax.axis_size("tm") * 4
    anywhere = pl.BlockSpec(memory_space=pl.ANY)
    inside = pl.BlockSpec(memory_space=pltpu.VMEM)
    results = pl.pallas_call(
        functools.partial(kernel, 1.0 / math.sqrt(count)),
        out_shape=(
            jax.ShapeDtypeStruct((2, ROWS, 4096), BF16),
            jax.ShapeDtypeStruct((2, 4, 4096), BF16),
            jax.ShapeDtypeStruct((2, 4, 4096), BF16),
            jax.ShapeDtypeStruct((CORES, PLANE, PIECE, 128), BF16),
        ),
        in_specs=[anywhere] * 4 + [inside] * 3,
        out_specs=(anywhere,) * 4,
        scratch_shapes=[
            pltpu.VMEM((6, ROWS, SPAN), BF16),
            pltpu.VMEM((6, ROWS, SPAN), BF16),
            pltpu.VMEM((2, ROWS, SPAN), BF16),
            pltpu.VMEM((6, FLAT + ROWS, 128), BF16),
            pltpu.VMEM((8, FLAT + ROWS, 128), BF16),
            pltpu.VMEM((6, 3, FLAT, 128), BF16),
            pltpu.VMEM((4, FLAT, 128), F32),
            pltpu.VMEM((4, FLAT, 128), F32),
            pltpu.VMEM((6, FLAT, 128), BF16),
            pltpu.VMEM((4, 3, FLAT, 128), BF16),
            pltpu.VMEM((8, FLAT + ROWS, 128), BF16),
            pltpu.VMEM((4, ROWS, SPAN), BF16),
            pltpu.VMEM((8, 2, 2, 4, SPAN), BF16),
            pltpu.VMEM((2, 2, 2, 4, HALF), BF16),
            pltpu.VMEM((768, 384), F32),
            pltpu.VMEM((384, 768), F32),
            pltpu.VMEM((768, 384), BF16),
            pltpu.VMEM((384, 768), BF16),
            pltpu.VMEM((384, 768), BF16),
            pltpu.VMEM((SUMS, 128), F32),
            pltpu.VMEM((PART, 128), F32),
            pltpu.VMEM((PLANE, PIECE, 128), BF16),
            pltpu.VMEM((PLANE, PIECE, 128), BF16),
            pltpu.VMEM((LINE, PIECE, 128), BF16),
            pltpu.VMEM((CORES, PLANE, PIECE, 128), BF16),
            pltpu.SemaphoreType.DMA((4,)),
            pltpu.SemaphoreType.DMA((PLANE,)),
            pltpu.SemaphoreType.DMA((PLANE,)),
            pltpu.SemaphoreType.DMA((LINE,)),
            pltpu.SemaphoreType.DMA((LINE,)),
            pltpu.SemaphoreType.DMA((PLANE,)),
            pltpu.SemaphoreType.DMA((PLANE,)),
            pltpu.SemaphoreType.DMA((2,)),
            pltpu.SemaphoreType.DMA((8,)),
            pltpu.SemaphoreType.DMA((22,)),
            pltpu.SemaphoreType.DMA((22,)),
            pltpu.SemaphoreType.DMA((YS,)),
            pltpu.SemaphoreType.DMA((2,)),
            pltpu.SemaphoreType.DMA((2,)),
            pltpu.SemaphoreType.DMA((2,)),
        ],
        compiler_params=pltpu.CompilerParams(
            collective_id=0, has_side_effects=True, vmem_limit_bytes=56 << 20
        ),
    )(
        block_input[0], input_cache[0], middle_cache[0], cotangent[0],
        first_weight.reshape(TAPS, 64, 64), second_weight.reshape(TAPS, 64, 64), first_bias.reshape(1, 64),
    )
    out, icg, mcg, grad1, grad2 = pl.pallas_call(
        deliver,
        out_shape=(
            jax.ShapeDtypeStruct((2, ROWS, 4096), BF16),
            jax.ShapeDtypeStruct((2, 4, 4096), BF16),
            jax.ShapeDtypeStruct((2, 4, 4096), BF16),
            jax.ShapeDtypeStruct((TAPS, 64, 64), F32),
            jax.ShapeDtypeStruct((TAPS, 64, 64), F32),
        ),
        in_specs=[anywhere] * 4,
        out_specs=(anywhere,) * 5,
        scratch_shapes=[
            pltpu.VMEM((2, ROWS, 4096), BF16),
            pltpu.VMEM((2, 4, 4096), BF16),
            pltpu.VMEM((2, 4, 4096), BF16),
            pltpu.VMEM((CORES, PLANE, PIECE, 128), BF16),
            pltpu.VMEM((TAPS, 64, 64), F32),
            pltpu.VMEM((TAPS, 64, 64), F32),
            pltpu.SemaphoreType.DMA((4,)),
            pltpu.SemaphoreType.DMA((9,)),
        ],
    )(*results)
    shape = (3, 3, 3, 64, 64)
    return (out[None], icg[None], mcg[None], grad1.reshape(shape), grad2.reshape(shape))


def solution(mesh):
    return jax.shard_map(
        body,
        mesh=mesh,
        in_specs=(
            P("clip", "tm", None, None),
            P("clip", None, None, None),
            P("clip", None, None, None),
            P(),
            P(),
            P(),
            P("clip", "tm", None, None),
        ),
        out_specs=(
            P("clip", "tm", None, None),
            P("clip", None, "tm", None),
            P("clip", None, "tm", None),
            P(),
            P(),
        ),
        check_vma=False,
    )
```

time: 91.4 us -> 73.8 us (0.81)
  Pallas kernels: 84.6 us -> 72.9 us
  local copies, waits for them, and re-layouts: 5.86 us -> 0 us
    pallas_call x1, Pallas kernels: 84.6 us -> 70.3 us  [body(): pl.pallas_call(functools.partial(kernel, 1.0 / math.sqrt(count)), out_sha...]
    unnamed x13 -> x0, local copies, waits for them, and re-layouts: 5.86 us -> none
    pallas_call x0 -> x1, Pallas kernels: none -> 2.57 us  [body(): pl.pallas_call(deliver, out_shape=(jax.ShapeDtypeStruct((2, ROWS, 4096),...]
where the time goes in v2:
time: 73.8 us; the launch traced here: 73.7 us
  Pallas kernels  72.9 us (99%)
  between operations  0.8 us (1%)
    pallas_call x1, Pallas kernels, body(): pl.pallas_call(functools.partial(kernel, 1.0 / math.sqrt(count)), out_sha...  70.3 us
    pallas_call x1, Pallas kernels, body(): pl.pallas_call(deliver, out_shape=(jax.ShapeDtypeStruct((2, ROWS, 4096),...  2.57 us

profile of v2, /device:TPU:1, one launch (start us, length us, event | category | flops | bytes accessed | tf_op | source)
XLA Modules:
  0.0 73.7 jit_solution(14634058315290996251)
XLA Ops:
  0.6 70.3 %shard_map.110 = (bf16[2,32,4096]{2,1,0:T(8,128)(2,1)}, bf16[2,4,4096]{2,1,0:T(4,128)(2,1)}, bf16[2,4,4096]{2,1,0:T(4,128)(2,1)}, bf16[2,16,56,128]{3,2,1,0:T(8,128)(2,1)}) custom-call(bf16[2,32,4096]{2,1,0:T(8,128)(2,1)} %bitcast.12, bf16[2,32,4096]{2,1,0:T(8,128)(2,1)} %bitcast.13, bf16[2,32,4096]{2,1,0:T(8,128)(2,1)} %bitcast.14, ...), custom_call_target="tpu_custom_call" | custom-call | tf_op jit(solution)/shard_map/pallas_call | solution.py:579
  71.0 2.6 %shard_map.111 = (bf16[2,32,4096]{2,1,0:T(8,128)(2,1)}, bf16[2,4,4096]{2,1,0:T(4,128)(2,1)}, bf16[2,4,4096]{2,1,0:T(4,128)(2,1)}, f32[27,64,64]{2,1,0:T(8,128)}, f32[27,64,64]{2,1,0:T(8,128)}) custom-call(bf16[2,32,4096]{2,1,0:T(8,128)(2,1)} %get-tuple-element.14.out_in, bf16[2,4,4096]{2,1,0:T(4,128)(2,1)} %get-tuple-element.15.icg_in, ...), custom_call_target="tpu_custom_call" | custom-call | tf_op jit(solution)/shard_map/pallas_call | solution.py:638

commit v3 on v2

--- a/solution.py
+++ b/solution.py
@@ -115,11 +115,11 @@
 
 def kernel(
     factor,
-    x_hbm, icache_hbm, mcache_hbm, ct_hbm, weight1, weight2, bias,
+    x_hbm, icache_hbm, mcache_hbm, ct_hbm, weight1_hbm, weight2_hbm, bias_hbm,
     out, icg, mcg, sums,
-    x, ct, mc, acts, cts, mid3, slope, mid_grad, pg, pg3, pgs, eg, dealt, passed, raw1, raw2,
+    weight1, weight2, bias, x, ct, mc, acts, cts, mid3, slope, mid_grad, pg, pg3, pgs, eg, dealt, passed, raw1, raw2,
     w1, w2t, w1t, vsum, from_core, plane_out, plane_in, line, whole,
-    core_sem, plane_send, plane_recv, line_send, line_recv, spread_send, spread_recv, leave_sem,
+    core_sem, plane_send, plane_recv, line_send, line_recv, spread_send, spread_recv, leave_sem, weight_sem,
     local_sem, send_sem, recv_sem, deal_sem, pass_send, pass_recv, own_sem,
 ):
     tm = lax.axis_index("tm")
@@ -128,15 +128,20 @@
     other = tm + 1 - 2 * side
     clip = lax.axis_index("clip")
     zlo, across, core = clip // (XS * CORES), (clip // CORES) % XS, clip % CORES
-    spot, depth = across * YS + four, zlo * 2 + side
+    spot, depth = across * YS + four, side * ZLO + zlo
+
+    hops = lambda d, size: min(d, size - d)
+    plane_steps = [(i, j) for i in range(XS) for j in range(YS) if i or j]
+    plane_steps.sort(key=lambda step: -hops(step[0], XS) - hops(step[1], YS))
+    line_steps = sorted(range(1, LINE), key=lambda step: -hops(step, LINE))
 
     def in_plane(i):
-        to = (spot + i) % PLANE
-        return to, {"clip": (zlo * XS + to // YS) * CORES + core, "tm": to % YS * 2 + side}
+        to_x, to_y = (across + plane_steps[i - 1][0]) % XS, (four + plane_steps[i - 1][1]) % YS
+        return to_x * YS + to_y, {"clip": (zlo * XS + to_x) * CORES + core, "tm": to_y * 2 + side}
 
     def in_line(i):
-        to = (depth + i) % LINE
-        return {"clip": (to // 2 * XS + across) * CORES + core, "tm": four * 2 + to % 2}
+        to = (depth + line_steps[i - 1]) % LINE
+        return {"clip": (to % ZLO * XS + across) * CORES + core, "tm": four * 2 + to // ZLO}
 
     def anyone(src, dst, send, recv, to):
         return pltpu.make_async_remote_copy(src, dst, send, recv, device_id=to, device_id_type=MESH)
@@ -220,6 +225,14 @@
         for copy in ct_halo:
             copy.start()
 
+    weights = [
+        pltpu.make_async_copy(src, dst, weight_sem.at[i])
+        for i, (src, dst) in enumerate(((weight1_hbm, weight1), (weight2_hbm, weight2), (bias_hbm, bias)))
+    ]
+    for copy in weights:
+        copy.start()
+    for copy in weights:
+        copy.wait()
     widen(w1, weight1)
     widen_back(w2t, weight2)
     widen_back(w1t, weight1)
@@ -428,10 +441,24 @@
             fold(range(14 * k, min(TAPS, 14 + 14 * k)))
 
 
-    loop(0, 2, input_gradient)
+    def shift_pg(s):
+        pgs[s + 2] = half_shift(pg[s].astype(F32))
+
+    def late_frames(send):
+        @pl.when(jnp.logical_not(last))
+        def _():
+            for copy in pg_halo:
+                copy.wait_recv()
+
+        loop(4, 6, shift_pg)
+        for t in range(2, 4):
+            loop(t, t + 1, input_gradient)
+            if send:
+                back[t - 2].start()
 
     @pl.when(side == 1)
     def _():
+        loop(0, 2, input_gradient)
         for copy in back:
             copy.start()
 
@@ -447,29 +474,10 @@
         plane_out[i] = part(to).astype(BF16)
         gathers.append(anyone(plane_out.at[i], plane_in.at[i], plane_send.at[i], plane_recv.at[i], device))
         gathers[-1].start()
-    @pl.when(jnp.logical_not(last))
-    def _():
-        for copy in pg_halo:
-            copy.wait_recv()
-
-    def shift_pg(s):
-        pgs[s + 2] = half_shift(pg[s].astype(F32))
-
-    loop(4, 6, shift_pg)
-    loop(2, 3, input_gradient)
-
     @pl.when(side == 0)
     def _():
-        back[0].start()
-
-    loop(3, 4, input_gradient)
-
-    @pl.when(side == 0)
-    def _():
-        back[1].start()
-
-    for copy in stay:
-        copy.start()
+        late_frames(True)
+
     @pl.when(first)
     def _():
         loop(0, 2, lambda n: pieces(0, n, conv(cts, [n], w2t)))
@@ -484,6 +492,16 @@
     line[depth] = total.astype(BF16)
     lines = [anyone(line.at[depth], line.at[depth], line_send.at[i], line_recv.at[i], in_line(i)) for i in range(1, LINE)]
     for copy in lines:
+        copy.start()
+    @pl.when(side == 0)
+    def _():
+        loop(0, 2, input_gradient)
+
+    @pl.when(side == 1)
+    def _():
+        late_frames(False)
+
+    for copy in stay:
         copy.start()
     for copy in lines:
         copy.wait_recv()
@@ -575,7 +593,6 @@
 def body(block_input, input_cache, middle_cache, first_weight, first_bias, second_weight, cotangent):
     count = 1024 * lax.axis_size("clip") * lax.axis_size("tm") * 4
     anywhere = pl.BlockSpec(memory_space=pl.ANY)
-    inside = pl.BlockSpec(memory_space=pltpu.VMEM)
     results = pl.pallas_call(
         functools.partial(kernel, 1.0 / math.sqrt(count)),
         out_shape=(
@@ -584,9 +601,12 @@
             jax.ShapeDtypeStruct((2, 4, 4096), BF16),
             jax.ShapeDtypeStruct((CORES, PLANE, PIECE, 128), BF16),
         ),
-        in_specs=[anywhere] * 4 + [inside] * 3,
+        in_specs=[anywhere] * 7,
         out_specs=(anywhere,) * 4,
         scratch_shapes=[
+            pltpu.VMEM((TAPS, 64, 64), BF16),
+            pltpu.VMEM((TAPS, 64, 64), BF16),
+            pltpu.VMEM((1, 64), F32),
             pltpu.VMEM((6, ROWS, SPAN), BF16),
             pltpu.VMEM((6, ROWS, SPAN), BF16),
             pltpu.VMEM((2, ROWS, SPAN), BF16),
@@ -620,6 +640,7 @@
             pltpu.SemaphoreType.DMA((PLANE,)),
             pltpu.SemaphoreType.DMA((PLANE,)),
             pltpu.SemaphoreType.DMA((2,)),
+            pltpu.SemaphoreType.DMA((3,)),
             pltpu.SemaphoreType.DMA((8,)),
             pltpu.SemaphoreType.DMA((22,)),
             pltpu.SemaphoreType.DMA((22,)),

time: 73.8 us -> 70.5 us (0.955)
  Pallas kernels: 72.9 us -> 69.5 us
    pallas_call x1, Pallas kernels: 70.3 us -> 67 us  [body(): pl.pallas_call(functools.partial(kernel, 1.0 / math.sqrt(count)), out_sha...]
where the time goes in v3:
time: 70.5 us; the launch traced here: 70.3 us
  Pallas kernels  69.5 us (99%)
  between operations  0.8 us (1%)
    pallas_call x1, Pallas kernels, body(): pl.pallas_call(functools.partial(kernel, 1.0 / math.sqrt(count)), out_sha...  67 us
    pallas_call x1, Pallas kernels, body(): pl.pallas_call(deliver, out_shape=(jax.ShapeDtypeStruct((2, ROWS, 4096),...  2.57 us

profile of v3, /device:TPU:1, one launch (start us, length us, event | category | flops | bytes accessed | tf_op | source)
XLA Modules:
  0.0 70.3 jit_solution(323661236368017546)
XLA Ops:
  0.6 67.0 %shard_map.110 = (bf16[2,32,4096]{2,1,0:T(8,128)(2,1)}, bf16[2,4,4096]{2,1,0:T(4,128)(2,1)}, bf16[2,4,4096]{2,1,0:T(4,128)(2,1)}, bf16[2,16,56,128]{3,2,1,0:T(8,128)(2,1)}) custom-call(bf16[2,32,4096]{2,1,0:T(8,128)(2,1)} %bitcast.12, bf16[2,32,4096]{2,1,0:T(8,128)(2,1)} %bitcast.13, bf16[2,32,4096]{2,1,0:T(8,128)(2,1)} %bitcast.14, ...), custom_call_target="tpu_custom_call" | custom-call | tf_op jit(solution)/shard_map/pallas_call | solution.py:596
  67.6 2.6 %shard_map.111 = (bf16[2,32,4096]{2,1,0:T(8,128)(2,1)}, bf16[2,4,4096]{2,1,0:T(4,128)(2,1)}, bf16[2,4,4096]{2,1,0:T(4,128)(2,1)}, f32[27,64,64]{2,1,0:T(8,128)}, f32[27,64,64]{2,1,0:T(8,128)}) custom-call(bf16[2,32,4096]{2,1,0:T(8,128)(2,1)} %get-tuple-element.14.out_in, bf16[2,4,4096]{2,1,0:T(4,128)(2,1)} %get-tuple-element.15.icg_in, ...), custom_call_target="tpu_custom_call" | custom-call | tf_op jit(solution)/shard_map/pallas_call | solution.py:659
